TPU v7x, 32 devices: a whole 2x2x4 slice. The times are simulated.
32 devices in a mesh: tok: 8 (over y, x, core), exp: 4 (over z).
Axes of the slice: x: 2, y: 2, z: 4, core: 2. Of those that a mesh axis runs over, the one named last changes fastest.
Arguments:
- expert_rows: bfloat16 [4, 2048, 4096], P('exp', 'tok'), may hold values from -480 to 480
- router_input: bfloat16 [2048, 4096], P(('tok', 'exp')), may hold values from -6 to 6
- router_weight: float32 [4096, 4], replicated, may hold values from -0.09375 to 0.09375
- assign: int32 [2048, 2], P(('tok', 'exp')), may hold values from 0 to 3, all different within a row
- targets: int32 [2048], P(('tok', 'exp')), may hold values from 0 to 15999
- head: bfloat16 [4096, 16000], P('tok', 'exp'), may hold values from -0.35 to 0.35
Outputs:
- token_loss: float32 [2048], P(('tok', 'exp'))
- router_grad: float32 [4096, 4], replicated
- mean_loss: float32 [], replicated
All inputs are finite; a program needn't handle non-finite values.
Results may differ from a plain program's by a relative error of at most 0.007.
Values may be sent and summed in bfloat16 or wider, within the bound.
A program may use at most 128 MiB of HBM per device.

v0:
```python
import math

import jax
import jax.numpy as jnp
from jax import lax
from jax.sharding import PartitionSpec as P


def shards(expert_rows, router_input, router_weight, assign, targets, head):
    experts = router_weight.shape[1]
    own_rows = router_input.shape[0]
    tokens_all = own_rows * lax.axis_size("tok") * lax.axis_size("exp")
    loss_scale = 1.0 / math.sqrt(tokens_all)
    inputs = router_input.astype(jnp.float32)
    gate_logits = jnp.dot(inputs, router_weight, precision=lax.Precision.HIGHEST)
    labels = jnp.arange(experts, dtype=jnp.int32)
    first_hot = (assign[:, 0:1] == labels[None, :]).astype(jnp.float32)
    second_hot = (assign[:, 1:2] == labels[None, :]).astype(jnp.float32)
    differ = first_hot - second_hot
    mix_share = jax.nn.sigmoid(jnp.sum(gate_logits * differ, axis=1))
    mixing = mix_share[:, None] * first_hot + (1.0 - mix_share)[:, None] * second_hot
    local_rows = lax.all_to_all(expert_rows, "exp", split_axis=1, concat_axis=0, tiled=True)
    local_wide = local_rows.astype(jnp.float32)
    mixed_own = jnp.sum(mixing.T[:, :, None] * local_wide, axis=0).astype(jnp.bfloat16)
    mixed_rows, group_targets = (
        lax.all_gather(mixed_own, "exp", axis=0, tiled=True),
        lax.all_gather(targets, "exp", axis=0, tiled=True),
    )
    shard_width = head.shape[1]
    full_head = lax.all_gather(head, "tok", axis=0, tiled=True)
    logits = jnp.dot(mixed_rows, full_head, preferred_element_type=jnp.float32)
    first_col = lax.axis_index("exp") * shard_width
    columns = first_col + jnp.arange(shard_width, dtype=jnp.int32)
    target_hit = group_targets[:, None] == columns[None, :]
    picked = jnp.sum(jnp.where(target_hit, logits, 0.0), axis=1)
    local_top = jnp.max(logits, axis=1)
    row_top = lax.pmax(local_top, "exp")
    exp_total, target_logit = lax.psum(
        (jnp.sum(jnp.exp(logits - row_top[:, None]), axis=1), picked), "exp"
    )
    log_total = row_top + jnp.log(exp_total)
    group_loss = log_total - target_logit
    own_loss = lax.dynamic_slice_in_dim(group_loss, lax.axis_index("exp") * own_rows, own_rows, 0)
    loss_sum = lax.psum(jnp.sum(own_loss), ("tok", "exp"))
    slope = (
        loss_scale * (jnp.exp(logits - log_total[:, None]) - target_hit.astype(jnp.float32))
    ).astype(jnp.bfloat16)
    hidden_slope = lax.psum_scatter(
        lax.dot_general(
            slope, full_head, (((1,), (1,)), ((), ())), preferred_element_type=jnp.float32
        ).astype(jnp.bfloat16),
        "exp",
        scatter_dimension=0,
        tiled=True,
    ).astype(jnp.float32)
    weight_slope = jnp.sum(hidden_slope[None, :, :] * local_wide, axis=2).T
    spread = jnp.sum(weight_slope * differ, axis=1) * mix_share * (1.0 - mix_share)
    gate_slope = spread[:, None] * differ
    router_part = jnp.dot(inputs.T, gate_slope, precision=lax.Precision.HIGHEST)
    router_sum = lax.psum(router_part, ("tok", "exp"))
    mean_loss = loss_sum / tokens_all
    return (own_loss, router_sum, mean_loss)


def solution(mesh):
    in_specs = (
        P("exp", "tok", None),
        P(("tok", "exp"), None),
        P(),
        P(("tok", "exp"), None),
        P(("tok", "exp")),
        P("tok", "exp"),
    )
    out_specs = (P(("tok", "exp")), P(), P())
    return jax.shard_map(shards, mesh=mesh, in_specs=in_specs, out_specs=out_specs, check_vma=False)
```

profile of v0, /device:TPU:0, one launch (start us, length us, event | category | flops | bytes accessed | tf_op | source)
XLA Modules:
  0.0 540.8 jit_solution(5459968139769704115)
XLA Ops:
  7.2 0.0 copy-start
  7.2 8.4 %copy.16 = bf16[1,256,4096]{2,0,1:T(2,128)(2,1)} copy(bf16[1,256,4096]{2,1,0:T(8,128)(2,1)} %param.6) | data formatting | bytes 4194304 | tf_op args[0]
  15.6 0.5 broadcast.107
  16.1 13.5 %reduce.1 = bf16[256,4096]{1,0:T(8,128)(2,1)S(1)} reduce(bf16[256,1,4096]{2,1,0:T(2,128)(2,1)} %bitcast.29, bf16[]{:T(256)} %broadcast.107), dimensions={1}, to_apply=%bitcast.25.reduce_sub_computation | reduce | bytes 4194306
  29.6 0.0 copy-start.3
  29.6 0.0 copy-start.2
  29.6 2.8 reshape.110
  32.4 6.3 %all-to-all-start = ((bf16[4,2,131072]{2,1,0:T(2,128)(2,1)}), bf16[4,2,131072]{2,1,0:T(2,128)(2,1)S(1)}, u32[]{:S(2)}, u32[]{:S(2)}) async-start(bf16[4,2,131072]{2,1,0:T(2,128)(2,1)} %reshape.110), calls=%async_computation | async-start | bytes 4194304 | tf_op jit(solution)/shard_map/all_to_all | solution.py:22
  38.8 0.0 all-gather.3.cloned.1.call-start
  38.8 0.0 copy-done.3
  38.8 0.0 copy-done
  38.8 0.0 copy-done.2
  38.8 0.5 fusion.10
  39.4 47.6 %all-to-all-done = bf16[4,2,131072]{2,1,0:T(2,128)(2,1)S(1)} async-done(((bf16[4,2,131072]{2,1,0:T(2,128)(2,1)}), bf16[4,2,131072]{2,1,0:T(2,128)(2,1)S(1)}, u32[]{:S(2)}, u32[]{:S(2)}) %all-to-all-start) | async-done | bytes 2097184 | tf_op jit(solution)/shard_map/all_to_all | solution.py:22
  87.0 3.3 reshape.111
  90.2 6.0 %copy_convert_fusion = f32[1,256,4096]{2,1,0:T(8,128)S(1)} fusion(bf16[1,256,4096]{2,0,1:T(2,128)(2,1)} %bitcast.27), kind=kLoop, calls=%fused_computation.12 | loop fusion | flops 1048576 | bytes 6291456 | tf_op jit(solution)/shard_map/convert_element_type | solution.py:23
  96.3 0.0 copy-start.5
  96.3 0.0 copy-start.4
  96.3 1.4 multiply_reduce_fusion
  97.7 0.0 all-gather.3.cloned.1.call-update
  97.7 0.0 all-gather.5.cloned.1.call-start
  97.7 0.7 all-gather.5.cloned.1.call-update
  98.4 0.2 reduce-scatter.2.cloned.1.call-start
  98.7 0.0 copy-done.5
  98.7 0.6 dynamic-slice
  99.9 0.0 copy-done.4
  99.9 0.2 dynamic-update-slice
  100.2 5.9 %all-reduce = s32[256]{0:T(256)S(1)} all-reduce(s32[256]{0:T(256)S(1)} %dynamic-update-slice), channel_id=1, replica_groups=mesh['tok'=8,'exp'=4] {'exp'}, use_global_device_ids=true, to_apply=%add | all-reduce | flops 256 | bytes 2048
  106.0 36.5 %all-gather.3.cloned.1.call-done = bf16[256,4096]{1,0:T(8,128)(2,1)} async-done(((bf16[64,4096]{1,0:T(8,128)(2,1)}), bf16[256,4096]{1,0:T(8,128)(2,1)}) %all-gather.3.cloned.1.call-update) | async-done | bytes 2097168 | tf_op jit(solution)/shard_map/all_gather | solution.py:26
  142.6 164.6 %all-gather.5.cloned.1.call-done = bf16[4096,4000]{0,1:T(8,128)(2,1)} async-done(((bf16[512,4000]{0,1:T(8,128)(2,1)}), bf16[4096,4000]{0,1:T(8,128)(2,1)}) %all-gather.5.cloned.1.call-update) | async-done | bytes 32768016 | tf_op jit(solution)/shard_map/all_gather | solution.py:30
  307.2 16.2 %fusion.19 = (f32[256]{0:T(256)S(1)}, f32[256,4000]{0,1:T(8,128)}) fusion(bf16[256,4096]{1,0:T(8,128)(2,1)} %all-gather.3.cloned.1.call-done, bf16[4096,4000]{0,1:T(8,128)(2,1)} %all-gather.5.cloned.1.call-done), kind=kOutput, calls=%fused_computation.41 | convolution fusion | flops 8389632000 | bytes 38962176 | tf_op jit(solution)/shard_map/dot_general | solution.py:31
  323.4 11.7 %pmax.7 = f32[256]{0:T(256)S(1)} all-reduce(f32[256]{0:T(256)S(1)} %get-tuple-element.15), channel_id=1, replica_groups=mesh['tok'=8,'exp'=4] {'exp'}, use_global_device_ids=true, to_apply=%region_3.4 | all-reduce | flops 256 | bytes 2048 | tf_op jit(solution)/shard_map/pmax | solution.py:37
  335.1 3.9 fusion.1
  339.0 8.4 %all-reduce.1 = (f32[256]{0:T(256)S(1)}, f32[256]{0:T(256)S(1)}) all-reduce(f32[256]{0:T(256)S(1)} %get-tuple-element.4, f32[256]{0:T(256)S(1)} %get-tuple-element.3), channel_id=1, replica_groups=mesh['tok'=8,'exp'=4] {'exp'}, use_global_device_ids=true, to_apply=%region_5.6 | all-reduce | flops 512 | bytes 4096 | tf_op jit(solution)/shard_map/psum | solution.py:38
  347.4 17.2 %convolution_convert_fusion = bf16[256,4096]{1,0:T(8,128)(2,1)} fusion(bf16[4096,4000]{0,1:T(8,128)(2,1)} %all-gather.5.cloned.1.call-done, f32[256,4000]{0,1:T(8,128)} %get-tuple-element.16, f32[256]{0:T(256)S(1)} %get-tuple-element.10, s32[256]{0:T(256)S(1)} %all-reduce, s32[4000]{0:T(1024)S(1)} %iota_add_fusion), kind=kOutput, calls=%fused_computation | convolution fusion | flops 8395800576 | bytes 38979200 | tf_op jit(solution)/shard_map/dot_general | solution.py:49
  364.5 0.0 reduce-scatter.2.cloned.1.call-update
  364.6 0.0 all-reduce.4.cloned.1.call-start
  364.6 42.4 %reduce-scatter.2.cloned.1.call-done = bf16[64,4096]{1,0:T(8,128)(2,1)} async-done(((bf16[256,4096]{1,0:T(8,128)(2,1)}), bf16[64,4096]{1,0:T(8,128)(2,1)}) %reduce-scatter.2.cloned.1.call-update) | async-done | bytes 524304 | tf_op jit(solution)/shard_map/reduce_scatter | solution.py:48
  407.0 1.7 mul.89
  408.7 0.7 copy-done.1
  409.4 2.4 fusion
  411.8 0.1 reduce_sum.70
  411.9 1.0 convolution_bitcast_fusion
  412.8 0.0 all-reduce.4.cloned.1.call-update
  412.9 1.2 fusion.17
  414.0 39.6 %psum.31 = f32[]{:T(128)} all-reduce(f32[]{:T(128)} %get-tuple-element.7), channel_id=1, replica_groups=mesh['tok'=8,'exp'=4] {'tok','exp'}, use_global_device_ids=true, to_apply=%region_13.14 | all-reduce | flops 1 | bytes 8 | tf_op jit(solution)/shard_map/psum | solution.py:44
  454.3 77.4 %all-reduce.4.cloned.1.call-done = f32[4096,4]{0,1:T(4,128)} async-done(((f32[4096,4]{0,1:T(4,128)}), f32[4096,4]{0,1:T(4,128)}) %all-reduce.4.cloned.1.call-update) | async-done | bytes 65552 | tf_op jit(solution)/shard_map/psum | solution.py:60
  531.7 1.5 copy.19
  (9 shorter events, 0.1 us)
Async XLA Ops:
  7.2 31.6 %copy-start = (bf16[64,4096]{1,0:T(8,128)(2,1)S(1)}, bf16[64,4096]{1,0:T(8,128)(2,1)}, u32[]{:S(2)}) copy-start(bf16[64,4096]{1,0:T(8,128)(2,1)} %param.7) | copy-start | bytes 1572868
  29.6 9.2 %copy-start.3 = (s32[64,2]{0,1:T(2,128)S(1)}, s32[64,2]{0,1:T(2,128)}, u32[]{:S(2)}) copy-start(s32[64,2]{0,1:T(2,128)} %param.9) | copy-start | bytes 1540
  29.6 9.2 %copy-start.2 = (f32[4096,4]{0,1:T(4,128)S(1)}, f32[4096,4]{0,1:T(4,128)}, u32[]{:S(2)}) copy-start(f32[4096,4]{0,1:T(4,128)} %param.8) | copy-start | bytes 196612
  32.4 54.5 %all-to-all-start = ((bf16[4,2,131072]{2,1,0:T(2,128)(2,1)}), bf16[4,2,131072]{2,1,0:T(2,128)(2,1)S(1)}, u32[]{:S(2)}, u32[]{:S(2)}) async-start(bf16[4,2,131072]{2,1,0:T(2,128)(2,1)} %reshape.110), calls=%async_computation | async-start | bytes 4194304 | tf_op jit(solution)/shard_map/all_to_all | solution.py:22
  38.8 103.8 %all-gather.3.cloned.1.call-start = ((), (), s32[]{:S(2)}) async-start(), calls=%async_computation.2 | async-start | bytes 2621440 | tf_op jit(solution)/shard_map/all_gather | solution.py:26
  96.3 2.4 copy-start.5
  96.3 3.6 copy-start.4
  97.7 209.5 %all-gather.5.cloned.1.call-start = ((), (), s32[]{:S(2)}) async-start(), calls=%async_computation.3 | async-start | bytes 36864000 | tf_op jit(solution)/shard_map/all_gather | solution.py:30
  98.4 308.6 %reduce-scatter.2.cloned.1.call-start = ((), (), s32[]{:S(2)}) async-start(), calls=%async_computation.4 | async-start | bytes 2621440 | tf_op jit(solution)/shard_map/reduce_scatter | solution.py:48
  364.6 167.1 %all-reduce.4.cloned.1.call-start = ((), (), s32[]{:S(2)}) async-start(), calls=%async_computation.5 | async-start | bytes 131072 | tf_op jit(solution)/shard_map/psum | solution.py:60
  407.0 2.3 copy-start.1
Sparse Core Ops, SparseCore 0:
  97.8 44.7 all-gather.2
  144.5 162.6 all-gather.4
  364.7 42.2 reduce-scatter.1
  413.0 118.5 all-reduce.3
where the time goes:
time: 543 us; the launch traced here: 541 us
  waiting for transfers between devices  369 us (68%)
  blocking collectives  65.5 us (12%)
  matrix products  34.9 us (6%)
  other arithmetic  28.4 us (5%)
  local copies, waits for them, and re-layouts  19.7 us (4%)
  between operations  16.3 us (3%)
  starting transfers between devices  6.65 us (1%)
    all_gather x1, waiting for transfers between devices, shards(): full_head = lax.all_gather(head, 'tok', axis=0, tiled=True)  165 us
    psum x1, waiting for transfers between devices, shards(): router_sum = lax.psum(router_part, ('tok', 'exp'))  77.4 us
    all_to_all x1, waiting for transfers between devices, shards(): lax.all_to_all(expert_rows, 'exp', split_axis=1, concat_axis=0, tiled=True)  47.6 us
    reduce_scatter x1, waiting for transfers between devices, shards(): lax.psum_scatter(lax.dot_general(slope, full_head, (((1,), (1,)), ((), ()...  42.4 us
    psum x1, blocking collectives, shards(): loss_sum = lax.psum(jnp.sum(own_loss), ('tok', 'exp'))  39.6 us
    all_gather x1, waiting for transfers between devices, shards(): lax.all_gather(mixed_own, 'exp', axis=0, tiled=True)  36.5 us
    unnamed x20, local copies, waits for them, and re-layouts  18 us
    dot_general x1, matrix products, shards(): lax.dot_general(slope, full_head, (((1,), (1,)), ((), ())), preferred_ele...  17.2 us
  transfers between devices with their start and end apart: 5, of which 5 were waited for; matrix products, arithmetic and copies ran while one was open for 0% of the time, Pallas kernels for 0%

commit v1 on v0

v1 whole, which is shorter than its diff:
```python
import functools
import math

import jax
import jax.numpy as jnp
from jax import lax
from jax.experimental import pallas as pl
from jax.experimental.pallas import tpu as pltpu
from jax.sharding import PartitionSpec as P

MESH = pl.DeviceIdType.MESH
F32 = jnp.float32
BF16 = jnp.bfloat16
TILE = 512


def plane(n_tok):
    chips = n_tok // 2
    ny = max(d for d in range(1, math.isqrt(chips) + 1) if chips % d == 0)
    return ny, chips // ny


def kernel(cfg, expert_ref, head_ref, x_ref, wt_ref, assign_ref, tgt_ref,
           loss_ref, grad_ref,
           wide, rows, mixed, drow, tgt, logits, slope, hid, hrecv, stat, part, part_in, chip_in, z_in, both,
           loc_sem, head_s, head_r, core_s, core_r, row_s, row_r, mix_s, mix_r, tgt_s, tgt_r, st_s, st_r,
           hid_s, hid_r, red_s, red_r, chip_s, chip_r, z_s, z_r):
    n_tok, n_exp, vocab, experts, tokens_all = cfg
    ny, nx = plane(n_tok)
    chips = ny * nx
    me, z = lax.axis_index("tok"), lax.axis_index("exp")
    chip, core = me // 2, lax.rem(me, 2)
    cy, cx = chip // nx, lax.rem(chip, nx)
    mate = chip * 2 + (1 - core)
    right_x = (cy * nx + lax.rem(cx + 1, nx)) * 2 + core
    right_y = (lax.rem(cy + 1, ny) * nx + cx) * 2 + core
    own, dim = x_ref.shape
    group = own * n_exp
    block, width = head_ref.shape
    half = block // 2
    tiles = width // TILE

    def slot(ry, rx, rc):
        return (ry * nx + rx) * 2 + rc

    def owner(ry, rx, rc):
        oy, ox = lax.rem(cy - ry + ny, ny), lax.rem(cx - rx + nx, nx)
        return (oy * nx + ox) * 2 + (core if rc == 0 else 1 - core)

    def remote(src, dst, send, recv, tok, exp):
        return pltpu.make_async_remote_copy(src_ref=src, dst_ref=dst, send_sem=send, recv_sem=recv,
                                            device_id=(tok, exp), device_id_type=MESH)

    sends = []

    def go(copy):
        copy.start()
        sends.append(copy)
        return copy

    incoming = {}
    core_in = {}

    def piece(ref, h):
        return ref.at[pl.ds(h * half, half), :]

    def forward(ry, rx, h):
        source = piece(head_ref, h) if (ry, rx) == (0, 0) else piece(wide.at[slot(ry, rx, 0)], h)
        hops = []
        if h == 0:
            if ry == 0 and rx < nx - 1:
                hops.append(("x", ry, rx + 1))
            if ry < ny - 1:
                hops.append(("y", ry + 1, rx))
        else:
            if rx == 0 and ry < ny - 1:
                hops.append(("y", ry + 1, rx))
            if rx < nx - 1:
                hops.append(("x", ry, rx + 1))
        for axis, ty, tx in hops:
            k = slot(ty, tx, 0)
            incoming[ty, tx, h] = go(remote(source, piece(wide.at[k], h), head_s.at[k, h], head_r.at[k, h],
                                            right_x if axis == "x" else right_y, z))
        k = slot(ry, rx, 1)
        core_in[ry, rx, h] = go(remote(source, piece(wide.at[k], h), core_s.at[k, h], core_r.at[k, h], mate, z))

    forward(0, 0, 0)
    forward(0, 0, 1)
    own_head = pltpu.make_async_copy(head_ref, wide.at[0], loc_sem.at[0])
    own_head.start()

    row_in, tgt_in = [], []
    mine = pl.ds(pl.multiple_of(z * own, own), own)
    for k in range(1, n_exp):
        peer = lax.rem(z + k, n_exp)
        theirs = pl.ds(pl.multiple_of(peer * own, own), own)
        row_in.append(go(remote(expert_ref.at[0, theirs, :], rows.at[z], row_s.at[k], row_r.at[k], me, peer)))
        tgt_in.append(go(remote(tgt_ref, tgt.at[mine, :], tgt_s.at[k], tgt_r.at[k], me, peer)))
    own_rows = pltpu.make_async_copy(expert_ref.at[0, mine, :], rows.at[z], loc_sem.at[1])
    own_rows.start()
    tgt[mine, :] = tgt_ref[...]

    def clear(i, _):
        logits[:, pl.ds(pl.multiple_of(i * TILE, TILE), TILE)] = jnp.zeros((group, TILE), F32)
        return 0

    lax.fori_loop(0, tiles, clear, 0)

    chosen = assign_ref[...]
    first = [(chosen[:, 0:1] == e).astype(F32) for e in range(experts)]
    second = [(chosen[:, 1:2] == e).astype(F32) for e in range(experts)]
    differ = [f - s for f, s in zip(first, second)]
    cols = TILE
    steps = dim // cols

    def gate_step(i, acc):
        at = pl.ds(pl.multiple_of(i * cols, cols), cols)
        x = x_ref[:, at].astype(F32)
        return tuple(a + jnp.sum(x * wt_ref[e:e + 1, at], axis=1, keepdims=True) for e, a in enumerate(acc))

    gates = lax.fori_loop(0, steps, gate_step, tuple(jnp.zeros((own, 1), F32) for _ in range(experts)))
    share = jax.nn.sigmoid(sum(g * d for g, d in zip(gates, differ)))
    mixing = [share * f + (1.0 - share) * s for f, s in zip(first, second)]

    own_rows.wait()
    for copy in row_in:
        copy.wait_recv()

    def mix_step(i, _):
        at = pl.ds(pl.multiple_of(i * cols, cols), cols)
        total = jnp.zeros((own, cols), F32)
        apart = jnp.zeros((own, cols), F32)
        for e in range(experts):
            r = rows[e, :, at].astype(F32)
            total = total + mixing[e] * r
            apart = apart + differ[e] * r
        mixed[mine, at] = total.astype(BF16)
        drow[:, at] = apart
        return 0

    lax.fori_loop(0, steps, mix_step, 0)
    mix_in = []
    for k in range(1, n_exp):
        peer = lax.rem(z + k, n_exp)
        mix_in.append(go(remote(mixed.at[mine, :], mixed.at[mine, :], mix_s.at[k], mix_r.at[k], me, peer)))
    for copy in mix_in + tgt_in:
        copy.wait_recv()

    def add_block(ry, rx, rc):
        k = slot(ry, rx, rc)
        left = mixed[:, pl.ds(pl.multiple_of(owner(ry, rx, rc) * block, block), block)]

        def step(i, _):
            at = pl.ds(pl.multiple_of(i * TILE, TILE), TILE)
            logits[:, at] += jnp.dot(left, wide[k, :, at], preferred_element_type=F32)
            return 0

        lax.fori_loop(0, tiles, step, 0)

    def add_mate(ry, rx):
        for h in range(2):
            core_in[ry, rx, h].wait_recv()
        add_block(ry, rx, 1)

    own_head.wait()
    add_block(0, 0, 0)
    add_mate(0, 0)
    order = sorted(
        ((ry, rx, h) for ry in range(ny) for rx in range(nx) for h in range(2) if ry + rx > 0),
        key=lambda p: (p[0] + p[1], p[0] if p[2] == 0 else p[1], p[2]),
    )
    here, ready = {}, []
    for ry, rx, h in order:
        incoming[ry, rx, h].wait_recv()
        forward(ry, rx, h)
        here[ry, rx] = here.get((ry, rx), 0) + 1
        if here[ry, rx] == 2:
            for pair in ready:
                add_mate(*pair)
            ready = [(ry, rx)]
            add_block(ry, rx, 0)
    for pair in ready:
        add_mate(*pair)

    lane = lax.broadcasted_iota(jnp.int32, (group, TILE), 1)
    low = jnp.float32(-3.0e38)

    def top_step(i, m):
        at = pl.ds(pl.multiple_of(i * TILE, TILE), TILE)
        v = jnp.where(lane + i * TILE < vocab, logits[:, at], low)
        return jnp.maximum(m, jnp.max(v, axis=1, keepdims=True))

    top = lax.fori_loop(0, tiles, top_step, jnp.full((group, 1), low, F32))
    wanted = tgt[:, 0:1] - z * vocab

    def hit_of(i):
        col = lane + i * TILE
        return jnp.logical_and(col == wanted, col < vocab)

    def sum_step(i, carry):
        s, p = carry
        at = pl.ds(pl.multiple_of(i * TILE, TILE), TILE)
        v = logits[:, at]
        e = jnp.where(lane + i * TILE < vocab, jnp.exp(v - top), 0.0)
        p = p + jnp.sum(jnp.where(hit_of(i), v, 0.0), axis=1, keepdims=True)
        logits[:, at] = e
        return s + jnp.sum(e, axis=1, keepdims=True), p

    zero = jnp.zeros((group, 1), F32)
    total, picked = lax.fori_loop(0, tiles, sum_step, (zero, zero))
    narrow = lax.broadcasted_iota(jnp.int32, (group, 128), 1)
    packed = jnp.where(narrow == 0, top, jnp.where(narrow == 1, total, jnp.where(narrow == 2, picked, 0.0)))
    stat[z] = packed.T[0:8, :]
    st_in = []
    for k in range(1, n_exp):
        peer = lax.rem(z + k, n_exp)
        st_in.append(go(remote(stat.at[z], stat.at[z], st_s.at[k], st_r.at[k], me, peer)))
    for copy in st_in:
        copy.wait_recv()
    stats = [stat[q] for q in range(n_exp)]
    row_top = functools.reduce(jnp.maximum, [s[0:1, :] for s in stats])
    exp_total = sum(s[1:2, :] * jnp.exp(s[0:1, :] - row_top) for s in stats)
    log_total = row_top + jnp.log(exp_total)
    loss = log_total - sum(s[2:3, :] for s in stats)
    loss_ref[...] = loss
    column = jnp.broadcast_to(log_total, (128, group)).T[:, 0:1]
    factor = jnp.exp(top - column)
    scale = 1.0 / math.sqrt(tokens_all)

    def slope_step(i, _):
        at = pl.ds(pl.multiple_of(i * TILE, TILE), TILE)
        slope[:, at] = (scale * (logits[:, at] * factor - hit_of(i).astype(F32))).astype(BF16)
        return 0

    lax.fori_loop(0, tiles, slope_step, 0)

    def hid_copy(k, j):
        peer = lax.rem(z + j, n_exp)
        return remote(hid.at[k, peer], hrecv.at[k, j], hid_s.at[k, j], hid_r.at[k, j], me, peer)

    def back_step(k, _):
        out = lax.dot_general(slope[...], wide[k], (((1,), (1,)), ((), ())), preferred_element_type=F32)
        hid[k] = out.astype(BF16).reshape(n_exp, own, block)
        for j in range(1, n_exp):
            hid_copy(k, j).start()
        return 0

    lax.fori_loop(0, n_tok, back_step, 0)

    acc = jnp.zeros((own, 1), F32)
    for ry in range(ny):
        for rx in range(nx):
            for rc in range(2):
                k = slot(ry, rx, rc)
                hidden = hid[k, z].astype(F32)
                for j in range(1, n_exp):
                    hid_copy(k, j).wait_recv()
                    hidden = hidden + hrecv[k, j].astype(F32)
                at = pl.ds(pl.multiple_of(owner(ry, rx, rc) * block, block), block)
                acc = acc + jnp.sum(hidden * drow[:, at], axis=1, keepdims=True)
    spread = acc * share * (1.0 - share)
    weights = [spread * d for d in differ]

    quarter = dim // 4
    loss_share = jnp.sum(loss, axis=1, keepdims=True) * (1.0 / n_exp)
    for c in range(2):
        for q in range(2):
            x = x_ref[:, (c * 2 + q) * quarter:(c * 2 + q + 1) * quarter].astype(F32)
            for e in range(experts):
                part[c, q * experts + e:q * experts + e + 1, 0:quarter] = jnp.sum(weights[e] * x, axis=0, keepdims=True)
        part[c, :, quarter:quarter + 128] = jnp.broadcast_to(loss_share, (2 * experts, 128))
    trade = go(remote(part.at[1 - core], part_in, red_s.at[0], red_r.at[0], mate, z))
    trade.wait_recv()
    chip_in[chip] = part[core] + part_in[...]
    copies = []
    for k in range(1, chips):
        there = lax.rem(chip + k, chips)
        copies.append(go(remote(chip_in.at[chip], chip_in.at[chip], chip_s.at[k], chip_r.at[k], there * 2 + core, z)))
    for copy in copies:
        copy.wait_recv()
    z_in[z] = sum(chip_in[k] for k in range(chips))
    copies = []
    for k in range(1, n_exp):
        peer = lax.rem(z + k, n_exp)
        copies.append(go(remote(z_in.at[z], z_in.at[z], z_s.at[k], z_r.at[k], me, peer)))
    for copy in copies:
        copy.wait_recv()
    both[core] = sum(z_in[k] for k in range(n_exp))
    trade = go(remote(both.at[core], both.at[core], red_s.at[1], red_r.at[1], mate, z))
    trade.wait_recv()
    grad_ref[...] = both[...]

    for copy in sends:
        copy.wait_send()

    def drain(k, _):
        for j in range(1, n_exp):
            hid_copy(k, j).wait_send()
        return 0

    lax.fori_loop(0, n_tok, drain, 0)


def shards(n_tok, n_exp, expert_rows, router_input, router_weight, assign, targets, head):
    experts = router_weight.shape[1]
    own, dim = router_input.shape
    group = own * n_exp
    tokens_all = own * n_tok * n_exp
    block, vocab = head.shape
    width = -(-vocab // TILE) * TILE
    head = jnp.pad(head, ((0, 0), (0, width - vocab)))
    wide_targets = jnp.broadcast_to(targets[:, None], (own, 128))
    quarter = dim // 4
    packed = (2 * experts, quarter + 128)
    vmem = pl.BlockSpec(memory_space=pltpu.VMEM)
    hbm = pl.BlockSpec(memory_space=pl.ANY)
    dma = pltpu.SemaphoreType.DMA
    chips = n_tok // 2
    loss, grad = pl.pallas_call(
        functools.partial(kernel, (n_tok, n_exp, vocab, experts, tokens_all)),
        out_shape=(jax.ShapeDtypeStruct((1, group), F32), jax.ShapeDtypeStruct((2,) + packed, F32)),
        in_specs=[hbm, hbm, vmem, vmem, vmem, vmem],
        out_specs=(vmem, vmem),
        scratch_shapes=[
            pltpu.VMEM((n_tok, block, width), BF16),
            pltpu.VMEM((experts, own, dim), BF16),
            pltpu.VMEM((group, dim), BF16),
            pltpu.VMEM((own, dim), F32),
            pltpu.VMEM((group, 128), jnp.int32),
            pltpu.VMEM((group, width), F32),
            pltpu.VMEM((group, width), BF16),
            pltpu.VMEM((n_tok, n_exp, own, block), BF16),
            pltpu.VMEM((n_tok, n_exp, own, block), BF16),
            pltpu.VMEM((n_exp, 8, group), F32),
            pltpu.VMEM((2,) + packed, F32),
            pltpu.VMEM(packed, F32),
            pltpu.VMEM((chips,) + packed, F32),
            pltpu.VMEM((n_exp,) + packed, F32),
            pltpu.VMEM((2,) + packed, F32),
            dma((2,)),
            dma((n_tok, 2)), dma((n_tok, 2)), dma((n_tok, 2)), dma((n_tok, 2)),
            dma((n_exp,)), dma((n_exp,)), dma((n_exp,)), dma((n_exp,)),
            dma((n_exp,)), dma((n_exp,)), dma((n_exp,)), dma((n_exp,)),
            dma((n_tok, n_exp)), dma((n_tok, n_exp)),
            dma((2,)), dma((2,)),
            dma((chips,)), dma((chips,)), dma((n_exp,)), dma((n_exp,)),
        ],
        compiler_params=pltpu.CompilerParams(has_side_effects=True, vmem_limit_bytes=62 * 1024 * 1024),
        name="router_step",
    )(expert_rows, head, router_input, router_weight.T, assign, wide_targets)
    own_loss = lax.dynamic_slice_in_dim(loss[0], lax.axis_index("exp") * own, own, 0)
    router_sum = grad[:, :, :quarter].reshape(2, 2, experts, quarter).transpose(0, 1, 3, 2).reshape(dim, experts)
    mean_loss = grad[0, 0, quarter] / tokens_all
    return (own_loss, router_sum, mean_loss)


def solution(mesh):
    in_specs = (
        P("exp", "tok", None),
        P(("tok", "exp"), None),
        P(),
        P(("tok", "exp"), None),
        P(("tok", "exp")),
        P("tok", "exp"),
    )
    out_specs = (P(("tok", "exp")), P(), P())
    body = functools.partial(shards, mesh.shape["tok"], mesh.shape["exp"])
    return jax.shard_map(body, mesh=mesh, in_specs=in_specs, out_specs=out_specs, check_vma=False)
```

time: 543 us -> 255 us (0.47)
  waiting for transfers between devices: 369 us -> 0 us
  Pallas kernels: 0 us -> 236 us
  blocking collectives: 65.5 us -> 0 us
  matrix products: 34.9 us -> 0 us
  other arithmetic: 28.4 us -> 0 us
  between operations: 16.3 us -> 2.42 us
  starting transfers between devices: 6.65 us -> 0 us
    pallas_call x0 -> x1, Pallas kernels: none -> 236 us  [shards(): pl.pallas_call(functools.partial(kernel, (n_tok, n_exp, vocab, experts, t...]
    all_gather x2 -> x0, waiting for transfers between devices: 201 us -> none  [the longest x1 165 us: shards(): full_head = lax.all_gather(head, 'tok', axis=0, tiled=True)]
    psum x1 -> x0, waiting for transfers between devices: 77.4 us -> none  [shards(): router_sum = lax.psum(router_part, ('tok', 'exp'))]
    psum x2 -> x0, blocking collectives: 48 us -> none  [the longest x1 39.6 us: shards(): loss_sum = lax.psum(jnp.sum(own_loss), ('tok', 'exp'))]
    all_to_all x1 -> x0, waiting for transfers between devices: 47.6 us -> none  [shards(): lax.all_to_all(expert_rows, 'exp', split_axis=1, concat_axis=0, tiled=True)]
    reduce_scatter x1 -> x0, waiting for transfers between devices: 42.4 us -> none  [shards(): lax.psum_scatter(lax.dot_general(slope, full_head, (((1,), (1,)), ((), ()...]
    dot_general x4 -> x0, matrix products: 34.9 us -> none  [the longest x1 17.2 us: shards(): lax.dot_general(slope, full_head, (((1,), (1,)), ((), ())), preferred_ele...]
    unnamed x1 -> x0, other arithmetic: 13.5 us -> none
  transfers between devices with their start and end apart: 5 -> 0, of which waited for: 5 -> 0; matrix products, arithmetic and copies ran while one was open for 0% -> 0% of each run, Pallas kernels for 0% -> 0%
where the time goes in v1:
time: 255 us; the launch traced here: 254 us
  Pallas kernels  236 us (93%)
  local copies, waits for them, and re-layouts  16.4 us (6%)
    pallas_call x1, Pallas kernels, shards(): pl.pallas_call(functools.partial(kernel, (n_tok, n_exp, vocab, experts, t...  236 us
    unnamed x6, local copies, waits for them, and re-layouts  7.16 us

profile of v1, /device:TPU:0, one launch (start us, length us, event | category | flops | bytes accessed | tf_op | source)
XLA Modules:
  0.0 254.3 jit_solution(6959752701599942296)
XLA Ops:
  0.6 6.4 %copy.9 = bf16[512,4000]{1,0:T(8,128)(2,1)} copy(bf16[512,4000]{0,1:T(8,128)(2,1)} %param.11) | data formatting | bytes 8192000 | tf_op args[5]
  7.1 0.0 copy-start
  7.1 0.0 copy-start.1
  7.1 4.7 %pad.4.head_ref = bf16[512,4096]{1,0:T(8,128)(2,1)} pad(bf16[512,4000]{1,0:T(8,128)(2,1)} %copy.9, bf16[]{:T(256)} %constant.5.clone.1), padding=0_0x0_96 | pad | bytes 8290306 | tf_op jit(solution)/shard_map/jit(_pad)/pad | solution.py:311
  11.8 0.0 copy-done
  11.8 0.7 copy.10.assign_ref
  12.5 0.0 copy-done.1
  12.5 0.7 broadcast_in_dim.2.tgt_ref
  13.2 235.5 %router_step.1 = (f32[1,256]{1,0:T(1,128)}, f32[2,8,1152]{2,1,0:T(8,128)}) custom-call(bf16[1,256,4096]{2,1,0:T(8,128)(2,1)} %expert_ref.1, bf16[512,4096]{1,0:T(8,128)(2,1)} %pad.4.head_ref, bf16[64,4096]{1,0:T(8,128)(2,1)} %x_ref.1, f32[4,4096]{1,0:T(4,128)} %bitcast.7, s32[64,2]{1,0:T(8,128)} %copy.10.assign_ref, s32[64,128]{1,0:T(8,128)} %broadcast_in_dim.2.tgt_ref), custom_call_target="tpu_custom_call" | custom-call | tf_op jit(solution)/shard_map/router_step/pallas_call | solution.py:319
  248.7 1.2 dynamic-slice_bitcast_fusion
  249.9 0.8 slice.6
  250.7 0.6 reshape.16
  251.4 1.2 slice.7
Async XLA Ops:
  7.1 4.7 %copy-start = (s32[64,2]{0,1:T(2,128)S(1)}, s32[64,2]{0,1:T(2,128)}, u32[]{:S(2)}) copy-start(s32[64,2]{0,1:T(2,128)} %param.9) | copy-start | bytes 1540
  7.1 5.4 %copy-start.1 = (s32[64]{0:T(128)S(1)}, s32[64]{0:T(128)}, u32[]{:S(2)}) copy-start(s32[64]{0:T(128)} %param.10) | copy-start | bytes 772

commit v2 on v1

--- a/solution.py
+++ b/solution.py
@@ -22,7 +22,7 @@
 
 def kernel(cfg, expert_ref, head_ref, x_ref, wt_ref, assign_ref, tgt_ref,
            loss_ref, grad_ref,
-           wide, rows, mixed, drow, tgt, logits, slope, hid, hrecv, stat, part, part_in, chip_in, z_in, both,
+           wide, rows, mixed, drow, tgt, logits, slope, hid, hrecv, relay, stat, part, part_in, chip_in, z_in, both,
            loc_sem, head_s, head_r, core_s, core_r, row_s, row_r, mix_s, mix_r, tgt_s, tgt_r, st_s, st_r,
            hid_s, hid_r, red_s, red_r, chip_s, chip_r, z_s, z_r):
     n_tok, n_exp, vocab, experts, tokens_all = cfg
@@ -36,8 +36,9 @@
     right_y = (lax.rem(cy + 1, ny) * nx + cx) * 2 + core
     own, dim = x_ref.shape
     group = own * n_exp
-    block, width = head_ref.shape
-    half = block // 2
+    block = head_ref.shape[1]
+    width = wide.shape[1]
+    split = vocab // 32 * 16
     tiles = width // TILE
 
     def slot(ry, rx, rc):
@@ -62,7 +63,7 @@
     core_in = {}
 
     def piece(ref, h):
-        return ref.at[pl.ds(h * half, half), :]
+        return ref.at[pl.ds(split, vocab - split), :] if h else ref.at[pl.ds(0, split), :]
 
     def forward(ry, rx, h):
         source = piece(head_ref, h) if (ry, rx) == (0, 0) else piece(wide.at[slot(ry, rx, 0)], h)
@@ -86,7 +87,7 @@
 
     forward(0, 0, 0)
     forward(0, 0, 1)
-    own_head = pltpu.make_async_copy(head_ref, wide.at[0], loc_sem.at[0])
+    own_head = pltpu.make_async_copy(head_ref, wide.at[0, pl.ds(0, vocab), :], loc_sem.at[0])
     own_head.start()
 
     row_in, tgt_in = [], []
@@ -105,6 +106,9 @@
         return 0
 
     lax.fori_loop(0, tiles, clear, 0)
+    if width > vocab:
+        for k in range(n_tok):
+            wide[k, vocab:width, :] = jnp.zeros((width - vocab, block), BF16)
 
     chosen = assign_ref[...]
     first = [(chosen[:, 0:1] == e).astype(F32) for e in range(experts)]
@@ -152,7 +156,8 @@
 
         def step(i, _):
             at = pl.ds(pl.multiple_of(i * TILE, TILE), TILE)
-            logits[:, at] += jnp.dot(left, wide[k, :, at], preferred_element_type=F32)
+            logits[:, at] += lax.dot_general(
+                left, wide[k, at, :], (((1,), (1,)), ((), ())), preferred_element_type=F32)
             return 0
 
         lax.fori_loop(0, tiles, step, 0)
@@ -238,14 +243,39 @@
         peer = lax.rem(z + j, n_exp)
         return remote(hid.at[k, peer], hrecv.at[k, j], hid_s.at[k, j], hid_r.at[k, j], me, peer)
 
+    ringed = n_exp == 4
+    near = (1, 3) if ringed else tuple(range(1, n_exp))
+    ahead, behind, far = lax.rem(z + 1, n_exp), lax.rem(z + n_exp - 1, n_exp), lax.rem(z + 2, n_exp)
+    low_half = own // 2
+
+    def relay_copy(k, side):
+        return remote(hid.at[k, far, pl.ds(side * low_half, low_half), :], relay.at[k, side],
+                      hid_s.at[k, 2 * side], hid_r.at[k, 2 * side], me, behind if side else ahead)
+
+    def pass_on(k):
+        for side, target in enumerate((ahead, behind)):
+            relay_copy(k, side).wait_recv()
+            at = pl.ds(side * low_half, low_half)
+            joined = hid[k, target, at, :].astype(F32) + relay[k, side].astype(F32)
+            hid[k, target, at, :] = joined.astype(BF16)
+        for j in near:
+            hid_copy(k, j).start()
+
     def back_step(k, _):
-        out = lax.dot_general(slope[...], wide[k], (((1,), (1,)), ((), ())), preferred_element_type=F32)
+        out = jnp.dot(slope[...], wide[k], preferred_element_type=F32)
         hid[k] = out.astype(BF16).reshape(n_exp, own, block)
-        for j in range(1, n_exp):
-            hid_copy(k, j).start()
+        if ringed:
+            for side in range(2):
+                relay_copy(k, side).start()
+            pl.when(k > 0)(lambda: pass_on(k - 1))
+        else:
+            for j in near:
+                hid_copy(k, j).start()
         return 0
 
     lax.fori_loop(0, n_tok, back_step, 0)
+    if ringed:
+        pass_on(n_tok - 1)
 
     acc = jnp.zeros((own, 1), F32)
     for ry in range(ny):
@@ -253,7 +283,7 @@
             for rc in range(2):
                 k = slot(ry, rx, rc)
                 hidden = hid[k, z].astype(F32)
-                for j in range(1, n_exp):
+                for j in near:
                     hid_copy(k, j).wait_recv()
                     hidden = hidden + hrecv[k, j].astype(F32)
                 at = pl.ds(pl.multiple_of(owner(ry, rx, rc) * block, block), block)
@@ -294,8 +324,11 @@
         copy.wait_send()
 
     def drain(k, _):
-        for j in range(1, n_exp):
+        for j in near:
             hid_copy(k, j).wait_send()
+        if ringed:
+            for side in range(2):
+                relay_copy(k, side).wait_send()
         return 0
 
     lax.fori_loop(0, n_tok, drain, 0)
@@ -308,7 +341,6 @@
     tokens_all = own * n_tok * n_exp
     block, vocab = head.shape
     width = -(-vocab // TILE) * TILE
-    head = jnp.pad(head, ((0, 0), (0, width - vocab)))
     wide_targets = jnp.broadcast_to(targets[:, None], (own, 128))
     quarter = dim // 4
     packed = (2 * experts, quarter + 128)
@@ -322,7 +354,7 @@
         in_specs=[hbm, hbm, vmem, vmem, vmem, vmem],
         out_specs=(vmem, vmem),
         scratch_shapes=[
-            pltpu.VMEM((n_tok, block, width), BF16),
+            pltpu.VMEM((n_tok, width, block), BF16),
             pltpu.VMEM((experts, own, dim), BF16),
             pltpu.VMEM((group, dim), BF16),
             pltpu.VMEM((own, dim), F32),
@@ -331,6 +363,7 @@
             pltpu.VMEM((group, width), BF16),
             pltpu.VMEM((n_tok, n_exp, own, block), BF16),
             pltpu.VMEM((n_tok, n_exp, own, block), BF16),
+            pltpu.VMEM((n_tok, 2, own // 2, block), BF16),
             pltpu.VMEM((n_exp, 8, group), F32),
             pltpu.VMEM((2,) + packed, F32),
             pltpu.VMEM(packed, F32),
@@ -347,7 +380,7 @@
         ],
         compiler_params=pltpu.CompilerParams(has_side_effects=True, vmem_limit_bytes=62 * 1024 * 1024),
         name="router_step",
-    )(expert_rows, head, router_input, router_weight.T, assign, wide_targets)
+    )(expert_rows, head.T, router_input, router_weight.T, assign, wide_targets)
     own_loss = lax.dynamic_slice_in_dim(loss[0], lax.axis_index("exp") * own, own, 0)
     router_sum = grad[:, :, :quarter].reshape(2, 2, experts, quarter).transpose(0, 1, 3, 2).reshape(dim, experts)
     mean_loss = grad[0, 0, quarter] / tokens_all

time: 255 us -> 235 us (0.922)
  Pallas kernels: 236 us -> 226 us
  local copies, waits for them, and re-layouts: 16.4 us -> 6.59 us
    pallas_call x1, Pallas kernels: 236 us -> 226 us  [shards(): pl.pallas_call(functools.partial(kernel, (n_tok, n_exp, vocab, experts, t...]
    unnamed x6 -> x1, local copies, waits for them, and re-layouts: 7.16 us -> 1.38 us
    pad x1 -> x0, local copies, waits for them, and re-layouts: 4.69 us -> none  [shards(): head = jnp.pad(head, ((0, 0), (0, width - vocab)))]
where the time goes in v2:
time: 235 us
  Pallas kernels  226 us (96%)
  local copies, waits for them, and re-layouts  6.59 us (3%)
  between operations  2.43 us (1%)
    pallas_call x1, Pallas kernels, shards(): pl.pallas_call(functools.partial(kernel, (n_tok, n_exp, vocab, experts, t...  226 us

profile of v2, /device:TPU:0, one launch (start us, length us, event | category | flops | bytes accessed | tf_op | source)
XLA Modules:
  0.0 234.9 jit_solution(10284849615248855935)
XLA Ops:
  0.6 1.4 copy.9.assign_ref
  2.0 1.3 broadcast_in_dim.2.tgt_ref
  3.4 225.9 %router_step.1 = (f32[1,256]{1,0:T(1,128)}, f32[2,8,1152]{2,1,0:T(8,128)}) custom-call(bf16[1,256,4096]{2,1,0:T(8,128)(2,1)} %expert_ref.1, bf16[4000,512]{1,0:T(8,128)(2,1)} %bitcast.8, bf16[64,4096]{1,0:T(8,128)(2,1)} %x_ref.1, f32[4,4096]{1,0:T(4,128)} %bitcast.10, s32[64,2]{1,0:T(8,128)} %copy.9.assign_ref, s32[64,128]{1,0:T(8,128)} %broadcast_in_dim.2.tgt_ref), custom_call_target="tpu_custom_call" | custom-call | tf_op jit(solution)/shard_map/router_step/pallas_call | solution.py:351
  229.2 1.2 slice.7
  231.1 1.2 dynamic-slice_bitcast_fusion
  232.3 0.8 slice.6
  233.1 0.6 reshape.16
